TPU v7x, 256 devices: a whole 4x4x8 slice. The times are simulated.
256 devices in a mesh: grp: 2 (over x_lo), blk: 128 (over x_hi, z, y, core).
Axes of the slice: x: 4 (x_hi: 2, x_lo: 2; x = x_hi * 2 + x_lo), y: 4, z: 8, core: 2. Of those that a mesh axis runs over, the one named last changes fastest.
Arguments:
- atoms: bfloat16 [131072, 512], P(('grp', 'blk')), parts along dimension 0, may hold values from -8 to 8
- edge_mask: int32 [256, 5, 512, 512], P(('grp', 'blk')), parts along dimension 0, may hold values from 0 to 1
- norm_gain: float32 [512], replicated, may hold values from 0.25 to 1.75
- w_query: bfloat16 [512, 512], replicated, may hold values from -3 to 3
- w_key: bfloat16 [512, 512], replicated, may hold values from -3 to 3
- w_value: bfloat16 [512, 512], replicated, may hold values from -0.25 to 0.25
- w_out: bfloat16 [512, 512], replicated, may hold values from -0.25 to 0.25
- bn_gain: float32 [512], replicated, may hold values from 0.25 to 1.75
- bn_shift: float32 [512], replicated, may hold values from -3 to 3
- w_up: bfloat16 [512, 1024], replicated, may hold values from -0.25 to 0.25
- w_down: bfloat16 [1024, 512], replicated, may hold values from -0.1875 to 0.1875
Outputs:
- updated: bfloat16 [131072, 512], P(('grp', 'blk')), parts along dimension 0
There are 2 independent parts, one for each index of `grp`. A program takes and returns all parts, laid end to end along the dimension named above; an argument that names none is the same for every part. Nothing has to cross between parts.
All inputs are finite; a program needn't handle non-finite values.
Results may differ from a plain program's by a relative error of at most 0.01.
The roundings to bfloat16 on the way count: a program that leaves them out, or rounds other values in their place, can miss the bound.
Values may be sent and summed in bfloat16 or wider, within the bound.
A program may use at most 128 MiB of HBM per device.

v0:
```python
import jax
import jax.numpy as jnp
from jax import lax
from jax.sharding import Mesh
from jax.sharding import PartitionSpec as P

D = 512
HEADS = 8
HEAD_DIM = 64
REACH = 2
BLK = ("blk_0", "blk_1", "blk_2", "blk_3")
GRP_BLK = ("grp", "blk_0", "blk_1", "blk_2", "blk_3")


def passed_along(value, axis, steps):
    count = lax.axis_size(axis)
    pairs = [(source, (source + steps) % count) for source in range(count)]
    return lax.ppermute(value, axis, pairs)


def one_axis_at_a_time(value, axes):
    for axis in axes:
        value = lax.psum(value, axis)
    return value


def attend_block(state, query_heads, kv_block, allowed):
    running_top, running_total, running_sum = state
    tile_rows = query_heads.shape[0]
    key_heads = kv_block[0].reshape(tile_rows, HEADS, HEAD_DIM)
    value_heads = kv_block[1].reshape(tile_rows, HEADS, HEAD_DIM)
    score = jnp.einsum(
        "qhd,khd->hqk", query_heads, key_heads, preferred_element_type=jnp.float32
    ) * HEAD_DIM ** (-0.5)
    score = jnp.where(allowed[None], score, -1e30)
    new_top = jnp.maximum(running_top, jnp.max(score, axis=-1))
    factor = jnp.exp(running_top - new_top)
    expo = jnp.exp(score - new_top[:, :, None])
    new_total = running_total * factor + jnp.sum(expo, axis=-1)
    product = jnp.einsum(
        "hqk,khd->qhd", expo.astype(jnp.bfloat16), value_heads, preferred_element_type=jnp.float32
    )
    new_sum = running_sum * jnp.transpose(factor)[:, :, None] + product
    return (new_top, new_total, new_sum)


def project_pair(features, w_key, w_value):
    keys = jnp.dot(features, w_key, preferred_element_type=jnp.float32).astype(jnp.bfloat16)
    values = jnp.dot(features, w_value, preferred_element_type=jnp.float32).astype(jnp.bfloat16)
    return jnp.stack([keys, values])


def body(
    atoms, edge_mask, norm_gain, w_query, w_key, w_value, w_out, bn_gain, bn_shift, w_up, w_down
):
    tile_rows = atoms.shape[0]
    xfull = atoms.astype(jnp.float32)
    normed = (
        xfull * lax.rsqrt(jnp.mean(xfull * xfull, axis=-1, keepdims=True) + 1e-06) * norm_gain
    ).astype(jnp.bfloat16)
    query = jnp.dot(normed, w_query, preferred_element_type=jnp.float32).astype(jnp.bfloat16)
    kv_own = project_pair(normed, w_key, w_value)
    query_heads = query.reshape(tile_rows, HEADS, HEAD_DIM)
    masks = edge_mask[0]
    diagonal = lax.broadcasted_iota(jnp.int32, (tile_rows, tile_rows), 0) == lax.broadcasted_iota(
        jnp.int32, (tile_rows, tile_rows), 1
    )
    state = (
        jnp.full((HEADS, tile_rows), -1e30, jnp.float32),
        jnp.zeros((HEADS, tile_rows), jnp.float32),
        jnp.zeros((tile_rows, HEADS, HEAD_DIM), jnp.float32),
    )
    state = attend_block(state, query_heads, kv_own, (masks[REACH] > 0) | diagonal)
    latest = {1: normed, -1: normed}
    for distance in range(1, REACH + 1):
        for sign in (1, -1):
            offset = sign * distance
            hop = -offset
            received = passed_along(normed, BLK, hop)
            kv_block = project_pair(received, w_key, w_value)
            latest[sign] = received
            state = attend_block(state, query_heads, kv_block, masks[offset + REACH] > 0)
    running_top, running_total, running_sum = state
    mixed = (
        (running_sum / jnp.transpose(running_total)[:, :, None])
        .reshape(tile_rows, D)
        .astype(jnp.bfloat16)
    )
    after = xfull + jnp.dot(mixed, w_out, preferred_element_type=jnp.float32)
    count = tile_rows * lax.axis_size(BLK)
    sums, squares = (
        one_axis_at_a_time(jnp.sum(after, axis=0), BLK),
        one_axis_at_a_time(jnp.sum(after * after, axis=0), BLK),
    )
    mean = sums / count
    var = squares / count - mean * mean
    centered = after - mean
    batched = (centered * lax.rsqrt(var + 1e-05) * bn_gain + bn_shift).astype(jnp.bfloat16)
    hidden = jax.nn.gelu(
        jnp.dot(batched, w_up, preferred_element_type=jnp.float32), approximate=True
    ).astype(jnp.bfloat16)
    return (after + jnp.dot(hidden, w_down, preferred_element_type=jnp.float32)).astype(
        jnp.bfloat16
    )


def solution(mesh):
    torus = Mesh(
        mesh.devices.reshape(mesh.shape["grp"], 2, 8, 4, 2),
        ("grp", "blk_0", "blk_1", "blk_2", "blk_3"),
    )
    return jax.shard_map(
        body,
        mesh=torus,
        in_specs=(
            P(GRP_BLK, None),
            P(GRP_BLK, None, None, None),
            P(),
            P(),
            P(),
            P(),
            P(),
            P(),
            P(),
            P(),
            P(),
        ),
        out_specs=P(GRP_BLK, None),
        check_vma=False,
    )
```

profile of v0, /device:TPU:1, one launch (start us, length us, event | category | flops | bytes accessed | tf_op | source)
XLA Modules:
  0.0 126.8 jit_solution(14850250318351792867)
XLA Ops:
  1.4 1.6 %fusion.83 = bf16[512,512]{1,0:T(8,128)(2,1)S(1)} fusion(bf16[512,512]{1,0:T(8,128)(2,1)} %param.11, f32[512]{0:T(512)} %param.13, f32[512]{0:T(512)S(1)} %add_rsqrt_fusion.1), kind=kLoop, calls=%fused_computation.76 | loop fusion | flops 1048576 | bytes 1052672 | tf_op jit(solution)/shard_map/convert_element_type | solution.py:60
  3.0 2.2 %collective-permute-start.3 = (bf16[512,512]{1,0:T(8,128)(2,1)S(1)}, bf16[512,512]{1,0:T(8,128)(2,1)}, u32[]{:S(2)}, u32[]{:S(2)}) collective-permute-start(bf16[512,512]{1,0:T(8,128)(2,1)S(1)} %fusion.83), channel_id=1, source_target_pairs={{0,2},{1,3},{2,4},{3,5},{4,6},{5,7},{6,8},{7,9},{8,10},{9,11},{10,... | collective-permute-start | bytes 1572872 | tf_op jit(solution)/shard_map/ppermute | solution.py:18
  5.2 9.3 %collective-permute-start.2 = (bf16[512,512]{1,0:T(8,128)(2,1)S(1)}, bf16[512,512]{1,0:T(8,128)(2,1)}, u32[]{:S(2)}, u32[]{:S(2)}) collective-permute-start(bf16[512,512]{1,0:T(8,128)(2,1)S(1)} %fusion.83), channel_id=1, source_target_pairs={{0,126},{1,127},{2,0},{3,1},{4,2},{5,3},{6,4},{7,5},{8,6},{9,7},{1... | collective-permute-start | bytes 1572872 | tf_op jit(solution)/shard_map/ppermute | solution.py:18
  15.5 2.3 %convolution_convert_fusion.8 = bf16[512,512]{0,1:T(8,128)(2,1)} fusion(bf16[512,512]{1,0:T(8,128)(2,1)S(1)} %fusion.83, bf16[512,512]{1,0:T(8,128)(2,1)} %param.16), kind=kOutput, calls=%fused_computation.71 | convolution fusion | flops 268697600 | bytes 1572864 | tf_op jit(solution)/shard_map/dot_general | solution.py:49
  17.8 2.3 %convolution_convert_fusion.9 = bf16[512,512]{0,1:T(8,128)(2,1)} fusion(bf16[512,512]{1,0:T(8,128)(2,1)S(1)} %fusion.83, bf16[512,512]{1,0:T(8,128)(2,1)} %param.15), kind=kOutput, calls=%fused_computation.72 | convolution fusion | flops 268697600 | bytes 1572864 | tf_op jit(solution)/shard_map/dot_general | solution.py:48
  28.4 2.6 %fusion = (f32[8,512]{1,0:T(8,128)S(1)}, f32[8,512,512]{1,2,0:T(8,128)S(1)}) fusion(pred[512,512]{0,1:T(8,128)(4,1)} %copy.12, bf16[512,8,64]{0,2,1:T(8,128)(2,1)S(1)} %bitcast.193, bf16[512,8,64]{0,2,1:T(8,128)(2,1)} %bitcast.198), kind=kOutput, calls=%fused_computation.10 | convolution fusion | flops 274722816 | bytes 9715712 | tf_op jit(solution)/shard_map/qhd,khd->hqk/dot_general | solution.py:32
  38.7 4.7 %fusion.1 = (f32[8,512]{1,0:T(8,128)S(1)}, f32[8,512,512]{1,2,0:T(8,128)}) fusion(pred[512,512]{0,1:T(8,128)(4,1)S(1)} %copy.14, bf16[512,8,64]{0,2,1:T(8,128)(2,1)S(1)} %bitcast.196, bf16[512,8,64]{0,2,1:T(8,128)(2,1)S(1)} %bitcast.202), kind=kOutput, calls=%fused_computation.11 | convolution fusion | flops 274722816 | bytes 9715712 | tf_op jit(solution)/shard_map/qhd,khd->hqk/dot_general | solution.py:32
  44.9 4.9 %fusion.2 = (f32[8,512]{1,0:T(8,128)S(1)}, f32[8,512,512]{1,2,0:T(8,128)}) fusion(pred[512,512]{0,1:T(8,128)(4,1)S(1)} %copy.16, bf16[512,8,64]{0,2,1:T(8,128)(2,1)S(1)} %bitcast.197, bf16[512,8,64]{0,2,1:T(8,128)(2,1)S(1)} %bitcast.199), kind=kOutput, calls=%fused_computation.12 | convolution fusion | flops 274722816 | bytes 9715712 | tf_op jit(solution)/shard_map/qhd,khd->hqk/dot_general | solution.py:32
  49.9 2.7 %fusion.13 = f32[8,512]{1,0:T(8,128)S(1)} fusion(f32[8,512,512]{1,2,0:T(8,128)S(1)} %get-tuple-element.33, f32[8,512]{1,0:T(8,128)S(1)} %get-tuple-element.19, pred[512,512]{0,1:T(8,128)(4,1)} %copy.20), kind=kLoop, calls=%fused_computation.23 | loop fusion | flops 8384512 | bytes 8683520 | tf_op jit(solution)/shard_map/reduce_sum | solution.py:39
  52.6 5.7 %fusion.9 = (f32[8,512]{1,0:T(8,128)S(1)}, f32[8,512]{1,0:T(8,128)S(1)}) fusion(f32[8,512,512]{1,2,0:T(8,128)} %get-tuple-element.37, f32[8,512]{1,0:T(8,128)S(1)} %get-tuple-element.21, pred[512,512]{0,1:T(8,128)(4,1)S(1)} %copy.16, f32[8,512]{1,0:T(8,128)S(1)} %get-tuple-element.20, f32[8,512,512]{1,2,0:T(8,128)S(1)} %get-tuple-element.35, ...), kind=kLoop, calls=%fused_computation.19 | loop fusion | flops 16769024 | bytes 17367040 | tf_op jit(solution)/shard_map/reduce_sum | solution.py:39
  58.3 5.7 %fusion.5 = (f32[8,512]{1,0:T(8,128)S(1)}, f32[8,512]{1,0:T(8,128)S(1)}) fusion(f32[8,512,512]{1,2,0:T(8,128)S(1)} %get-tuple-element.41, f32[8,512]{1,0:T(8,128)S(1)} %get-tuple-element.29, pred[512,512]{0,1:T(8,128)(4,1)S(1)} %copy-done.4, f32[8,512]{1,0:T(8,128)S(1)} %get-tuple-element.22, f32[8,512,512]{1,2,0:T(8,128)} %get-tuple-element.39, ...), kind=kLoop, calls=%fused_computation.15 | loop fusion | flops 16769024 | bytes 17367040 | tf_op jit(solution)/shard_map/reduce_sum | solution.py:39
  64.1 2.3 %fusion.68 = f32[512,8,64]{0,2,1:T(8,128)S(1)} fusion(bf16[512,8,64]{0,2,1:T(8,128)(2,1)S(1)} %bitcast.203, f32[8,512,512]{1,2,0:T(8,128)S(1)} %get-tuple-element.41, f32[8,512]{1,0:T(8,128)S(1)} %get-tuple-element.29, pred[512,512]{0,1:T(8,128)(4,1)S(1)} %copy-done.4, f32[512,8]{0,1:T(8,128)S(1)} %get-tuple-element.27, f32[512,8]{0,1:T(8,128)S(1)} %get-tuple-element.28), kind=kOutput, calls=%fused_computation.58 | convolution fusion | flops 277348352 | bytes 10272768 | tf_op jit(solution)/shard_map/hqk,khd->qhd/dot_general | solution.py:40
  66.5 1.7 %convolution_convert_fusion.6 = bf16[512,512]{0,1:T(8,128)(2,1)S(1)} fusion(bf16[512,512]{1,0:T(8,128)(2,1)} %collective-permute-done, bf16[512,512]{1,0:T(8,128)(2,1)S(1)} %copy-done.2), kind=kOutput, calls=%fused_computation.69 | convolution fusion | flops 268697600 | bytes 1572864 | tf_op jit(solution)/shard_map/dot_general | solution.py:49
  68.2 5.8 %fusion.71 = f32[512,8,64]{0,2,1:T(8,128)S(1)} fusion(f32[512,8,64]{0,2,1:T(8,128)S(1)} %fusion.68, bf16[512,8,64]{0,2,1:T(8,128)(2,1)S(1)} %bitcast.205, f32[8,512,512]{1,2,0:T(8,128)} %get-tuple-element.39, f32[8,512]{1,0:T(8,128)S(1)} %get-tuple-element.22, pred[512,512]{0,1:T(8,128)(4,1)S(1)} %copy.14, f32[512,8]{0,1:T(8,128)S(1)} %get-tuple-element.18), kind=kOutput, calls=%fused_computation.59 | convolution fusion | flops 277348352 | bytes 11304960 | tf_op jit(solution)/shard_map/hqk,khd->qhd/dot_general | solution.py:40
  75.5 2.3 %fusion.74 = f32[512,8,64]{0,2,1:T(8,128)S(1)} fusion(f32[512,8,64]{0,2,1:T(8,128)S(1)} %fusion.71, bf16[512,8,64]{0,2,1:T(8,128)(2,1)S(1)} %bitcast.206, f32[8,512,512]{1,2,0:T(8,128)S(1)} %bitcast.192, f32[8,512]{1,0:T(8,128)S(1)} %get-tuple-element.21, pred[512,512]{0,1:T(8,128)(4,1)S(1)} %copy.16, f32[512,8]{0,1:T(8,128)S(1)} %get-tuple-element.17), kind=kOutput, calls=%fused_computation.60 | convolution fusion | flops 277348352 | bytes 11304960 | tf_op jit(solution)/shard_map/hqk,khd->qhd/dot_general | solution.py:40
  77.8 1.6 %convolution_convert_fusion.2 = bf16[512,512]{0,1:T(8,128)(2,1)S(1)} fusion(bf16[512,512]{1,0:T(8,128)(2,1)} %collective-permute-done.2, bf16[512,512]{1,0:T(8,128)(2,1)S(1)} %copy-done.2), kind=kOutput, calls=%fused_computation.65 | convolution fusion | flops 268697600 | bytes 1572864 | tf_op jit(solution)/shard_map/dot_general | solution.py:49
  79.4 2.6 %fusion.77 = f32[512,8,64]{0,2,1:T(8,128)S(1)} fusion(f32[512,8,64]{0,2,1:T(8,128)S(1)} %fusion.74, bf16[512,8,64]{0,2,1:T(8,128)(2,1)S(1)} %bitcast.207, f32[8,512,512]{1,2,0:T(8,128)S(1)} %get-tuple-element.35, f32[8,512]{1,0:T(8,128)S(1)} %get-tuple-element.20, pred[512,512]{0,1:T(8,128)(4,1)S(1)} %copy.18, f32[512,8]{0,1:T(8,128)S(1)} %get-tuple-element.16), kind=kOutput, calls=%fused_computation.61 | convolution fusion | flops 277348352 | bytes 11304960 | tf_op jit(solution)/shard_map/hqk,khd->qhd/dot_general | solution.py:40
  82.0 1.6 %convolution_convert_fusion = bf16[512,512]{0,1:T(8,128)(2,1)S(1)} fusion(bf16[512,512]{1,0:T(8,128)(2,1)} %collective-permute-done.3, bf16[512,512]{1,0:T(8,128)(2,1)S(1)} %copy-done.2), kind=kOutput, calls=%fused_computation.63 | convolution fusion | flops 268697600 | bytes 1572864 | tf_op jit(solution)/shard_map/dot_general | solution.py:49
  83.7 2.4 %divide_convert_fusion = bf16[512,8,64]{0,2,1:T(8,128)(2,1)S(1)} fusion(f32[512,8,64]{0,2,1:T(8,128)S(1)} %fusion.77, bf16[512,8,64]{0,2,1:T(8,128)(2,1)S(1)} %bitcast.204, f32[8,512,512]{1,2,0:T(8,128)S(1)} %get-tuple-element.33, f32[8,512]{1,0:T(8,128)S(1)} %get-tuple-element.19, pred[512,512]{0,1:T(8,128)(4,1)S(1)} %copy-done.6, ...), kind=kOutput, calls=%fused_computation.82 | convolution fusion | flops 277610496 | bytes 10780672 | tf_op jit(solution)/shard_map/hqk,khd->qhd/dot_general | solution.py:40
  86.6 5.3 %all-reduce.3 = (f32[512]{0:T(512)S(1)}, f32[512]{0:T(512)S(1)}) all-reduce(f32[512]{0:T(512)S(1)} %get-tuple-element.6, f32[512]{0:T(512)S(1)} %get-tuple-element.5), channel_id=1, replica_groups=mesh['grp'=2,'blk_0'=2,'blk_1'=8,'blk_2'=4,'blk_3'=2] {'blk_0'}, use_global_device_ids=true, to_apply=%region_17.18 | all-reduce | flops 1024 | bytes 8192 | tf_op jit(solution)/shard_map/psum | solution.py:23
  91.9 10.7 %all-reduce = (f32[512]{0:T(512)S(1)}, f32[512]{0:T(512)S(1)}) all-reduce(f32[512]{0:T(512)S(1)} %get-tuple-element.13, f32[512]{0:T(512)S(1)} %get-tuple-element.14), channel_id=1, replica_groups=mesh['grp'=2,'blk_0'=2,'blk_1'=8,'blk_2'=4,'blk_3'=2] {'blk_1'}, use_global_device_ids=true, to_apply=%region_18.19 | all-reduce | flops 1024 | bytes 8192 | tf_op jit(solution)/shard_map/psum | solution.py:23
  102.6 11.0 %all-reduce.1 = (f32[512]{0:T(512)S(1)}, f32[512]{0:T(512)S(1)}) all-reduce(f32[512]{0:T(512)S(1)} %get-tuple-element.7, f32[512]{0:T(512)S(1)} %get-tuple-element.8), channel_id=1, replica_groups=mesh['grp'=2,'blk_0'=2,'blk_1'=8,'blk_2'=4,'blk_3'=2] {'blk_2'}, use_global_device_ids=true, to_apply=%region_19.20 | all-reduce | flops 1024 | bytes 8192 | tf_op jit(solution)/shard_map/psum | solution.py:23
  113.6 10.9 %all-reduce.2 = (f32[512]{0:T(512)S(1)}, f32[512]{0:T(512)S(1)}) all-reduce(f32[512]{0:T(512)S(1)} %get-tuple-element.9, f32[512]{0:T(512)S(1)} %get-tuple-element.10), channel_id=1, replica_groups=mesh['grp'=2,'blk_0'=2,'blk_1'=8,'blk_2'=4,'blk_3'=2] {'blk_3'}, use_global_device_ids=true, to_apply=%region_20.21 | all-reduce | flops 1024 | bytes 8192 | tf_op jit(solution)/shard_map/psum | solution.py:23
  124.5 2.2 %fusion.80 = bf16[512,512]{1,0:T(8,128)(2,1)} fusion(f32[512,512]{1,0:T(8,128)S(1)} %get-tuple-element.42, bf16[1024,512]{1,0:T(8,128)(2,1)S(1)} %copy-done, bf16[512,1024]{1,0:T(8,128)(2,1)S(1)} %copy-done.9, f32[512]{0:T(512)S(1)} %copy-done.11, f32[512]{0:T(512)S(1)} %copy-done.12, f32[512]{0:T(512)S(1)} %get-tuple-element.31, f32[512]{0:T(512)S(1)} %get-tuple-element.30), kind=kOutput, calls=%fused_computation.62 | convolution fusion | flops 1080295424 | bytes 3678208 | tf_op jit(solution)/shard_map/dot_general | solution.py:102
  (58 shorter events, 21.9 us)
Async XLA Ops:
  0.0 124.5 %copy-start = (bf16[1024,512]{1,0:T(8,128)(2,1)S(1)}, bf16[1024,512]{1,0:T(8,128)(2,1)}, u32[]{:S(2)}) copy-start(bf16[1024,512]{1,0:T(8,128)(2,1)} %param.21) | copy-start | bytes 3145732
  0.0 21.6 %copy-start.3 = (s32[1,5,512,512]{3,2,1,0:T(8,128)S(1)}, s32[1,5,512,512]{3,2,1,0:T(8,128)}, u32[]{:S(2)}) copy-start(s32[1,5,512,512]{3,2,1,0:T(8,128)} %param.12) | copy-start | bytes 15728644
  3.0 31.1 %collective-permute-start.3 = (bf16[512,512]{1,0:T(8,128)(2,1)S(1)}, bf16[512,512]{1,0:T(8,128)(2,1)}, u32[]{:S(2)}, u32[]{:S(2)}) collective-permute-start(bf16[512,512]{1,0:T(8,128)(2,1)S(1)} %fusion.83), channel_id=1, source_target_pairs={{0,2},{1,3},{2,4},{3,5},{4,6},{5,7},{6,8},{7,9},{8,10},{9,11},{10,... | collective-permute-start | bytes 1572872 | tf_op jit(solution)/shard_map/ppermute | solution.py:18
  5.2 25.8 %collective-permute-start.2 = (bf16[512,512]{1,0:T(8,128)(2,1)S(1)}, bf16[512,512]{1,0:T(8,128)(2,1)}, u32[]{:S(2)}, u32[]{:S(2)}) collective-permute-start(bf16[512,512]{1,0:T(8,128)(2,1)S(1)} %fusion.83), channel_id=1, source_target_pairs={{0,126},{1,127},{2,0},{3,1},{4,2},{5,3},{6,4},{7,5},{8,6},{9,7},{1... | collective-permute-start | bytes 1572872 | tf_op jit(solution)/shard_map/ppermute | solution.py:18
  14.5 28.9 %collective-permute-start.1 = (bf16[512,512]{1,0:T(8,128)(2,1)S(1)}, bf16[512,512]{1,0:T(8,128)(2,1)}, u32[]{:S(2)}, u32[]{:S(2)}) collective-permute-start(bf16[512,512]{1,0:T(8,128)(2,1)S(1)} %fusion.83), channel_id=1, source_target_pairs={{0,1},{1,2},{2,3},{3,4},{4,5},{5,6},{6,7},{7,8},{8,9},{9,10},{10,1... | collective-permute-start | bytes 1572872 | tf_op jit(solution)/shard_map/ppermute | solution.py:18
  14.5 22.7 %collective-permute-start = (bf16[512,512]{1,0:T(8,128)(2,1)S(1)}, bf16[512,512]{1,0:T(8,128)(2,1)}, u32[]{:S(2)}, u32[]{:S(2)}) collective-permute-start(bf16[512,512]{1,0:T(8,128)(2,1)S(1)} %fusion.83), channel_id=1, source_target_pairs={{0,127},{1,0},{2,1},{3,2},{4,3},{5,4},{6,5},{7,6},{8,7},{9,8},{10,... | collective-permute-start | bytes 1572872 | tf_op jit(solution)/shard_map/ppermute | solution.py:18
  21.7 9.4 %copy-start.1 = (bf16[512,512]{1,0:T(8,128)(2,1)S(1)}, bf16[512,512]{1,0:T(8,128)(2,1)}, u32[]{:S(2)}) copy-start(bf16[512,512]{1,0:T(8,128)(2,1)} %param.15) | copy-start | bytes 1572868
  31.0 4.7 %copy-start.5 = (pred[512,512]{0,1:T(8,128)(4,1)S(1)}, pred[512,512]{0,1:T(8,128)(4,1)}, u32[]{:S(2)}) copy-start(pred[512,512]{0,1:T(8,128)(4,1)} %copy.20) | copy-start | bytes 786436
  52.6 5.7 %copy-start.4 = (pred[512,512]{0,1:T(8,128)(4,1)S(1)}, pred[512,512]{0,1:T(8,128)(4,1)}, u32[]{:S(2)}) copy-start(pred[512,512]{0,1:T(8,128)(4,1)} %copy.12) | copy-start | bytes 786436
  58.3 5.8 %copy-start.8 = (bf16[512,512]{0,1:T(8,128)(2,1)S(1)}, bf16[512,512]{0,1:T(8,128)(2,1)}, u32[]{:S(2)}) copy-start(bf16[512,512]{0,1:T(8,128)(2,1)} %convolution_convert_fusion.8) | copy-start | bytes 1572868
  64.1 2.4 %copy-start.2 = (bf16[512,512]{1,0:T(8,128)(2,1)S(1)}, bf16[512,512]{1,0:T(8,128)(2,1)}, u32[]{:S(2)}) copy-start(bf16[512,512]{1,0:T(8,128)(2,1)} %param.16) | copy-start | bytes 1572868
  66.5 9.0 %slice-start = ((s8[8388608]{0:T(1024)(128)(4,1)}), s8[4194304]{0:T(1024)(128)(4,1)S(1)}, s32[]{:S(2)}) async-start(s8[8388608]{0:T(1024)(128)(4,1)} %bitcast.191), calls=%async_computation | async-start | bytes 8388608
  68.1 7.3 %slice-start.1 = ((s8[8388608]{0:T(1024)(128)(4,1)}), s8[4194304]{0:T(1024)(128)(4,1)S(1)}, s32[]{:S(2)}) async-start(s8[8388608]{0:T(1024)(128)(4,1)} %bitcast.191), calls=%async_computation.1 | async-start | bytes 8388608
  77.8 5.8 %copy-start.6 = (pred[512,512]{0,1:T(8,128)(4,1)S(1)}, pred[512,512]{0,1:T(8,128)(4,1)}, u32[]{:S(2)}) copy-start(pred[512,512]{0,1:T(8,128)(4,1)} %copy.20) | copy-start | bytes 786436
  82.0 4.1 %copy-start.7 = (bf16[512,512]{1,0:T(8,128)(2,1)S(1)}, bf16[512,512]{1,0:T(8,128)(2,1)}, u32[]{:S(2)}) copy-start(bf16[512,512]{1,0:T(8,128)(2,1)} %param.11) | copy-start | bytes 1572868
  82.0 4.1 %copy-start.10 = (bf16[512,512]{1,0:T(8,128)(2,1)S(1)}, bf16[512,512]{1,0:T(8,128)(2,1)}, u32[]{:S(2)}) copy-start(bf16[512,512]{1,0:T(8,128)(2,1)} %param.17) | copy-start | bytes 1572868
  83.6 40.9 %copy-start.9 = (bf16[512,1024]{1,0:T(8,128)(2,1)S(1)}, bf16[512,1024]{1,0:T(8,128)(2,1)}, u32[]{:S(2)}) copy-start(bf16[512,1024]{1,0:T(8,128)(2,1)} %param.20) | copy-start | bytes 3145732
  83.6 40.9 %copy-start.11 = (f32[512]{0:T(512)S(1)}, f32[512]{0:T(512)}, u32[]{:S(2)}) copy-start(f32[512]{0:T(512)} %param.19) | copy-start | bytes 6148
  83.7 40.9 %copy-start.12 = (f32[512]{0:T(512)S(1)}, f32[512]{0:T(512)}, u32[]{:S(2)}) copy-start(f32[512]{0:T(512)} %param.18) | copy-start | bytes 6148
where the time goes:
time: 127 us
  matrix products  52 us (41%)
  blocking collectives  37.9 us (30%)
  other arithmetic  18.7 us (15%)
  starting transfers between devices  12.4 us (10%)
  local copies, waits for them, and re-layouts  5.27 us (4%)
    psum x4, blocking collectives, one_axis_at_a_time(): value = lax.psum(value, axis)  37.9 us
    dot_general x5, matrix products, attend_block(): jnp.einsum('hqk,khd->qhd', expo.astype(jnp.bfloat16), value_heads, prefer...  15.4 us
    dot_general x5, matrix products, attend_block(): jnp.einsum('qhd,khd->hqk', query_heads, key_heads, preferred_element_type...  15.2 us
    reduce_sum x3, other arithmetic, attend_block(): new_total = running_total * factor + jnp.sum(expo, axis=-1)  14.1 us
    ppermute x4, starting transfers between devices, passed_along(): return lax.ppermute(value, axis, pairs)  12.4 us
    dot_general x5, matrix products, project_pair(): jnp.dot(features, w_value, preferred_element_type=jnp.float32)  8.7 us
    dot_general x5, matrix products, project_pair(): jnp.dot(features, w_key, preferred_element_type=jnp.float32)  8.45 us
    gt x4, local copies, waits for them, and re-layouts, body(): masks[offset + REACH] > 0  4.14 us
  transfers between devices with their start and end apart: 4, of which 0 were waited for; matrix products, arithmetic and copies ran while one was open for 22% of the time, Pallas kernels for 0%

commit v1 on v0

--- a/solution.py
+++ b/solution.py
@@ -20,7 +20,7 @@
 
 def one_axis_at_a_time(value, axes):
     for axis in axes:
-        value = lax.psum(value, axis)
+        value = jnp.sum(lax.all_gather(value, axis), axis=0)
     return value
 
 

time: 127 us -> 176 us (1.39)
  blocking collectives: 37.9 us -> 86.2 us
    all_gather x0 -> x8, blocking collectives: none -> 86.2 us  [one_axis_at_a_time(): value = jnp.sum(lax.all_gather(value, axis), axis=0)]
    psum x4 -> x0, blocking collectives: 37.9 us -> none  [one_axis_at_a_time(): value = lax.psum(value, axis)]
  transfers between devices with their start and end apart: 4 -> 4, of which waited for: 0 -> 0; matrix products, arithmetic and copies ran while one was open for 22% -> 16% of each run, Pallas kernels for 0% -> 0%
where the time goes in v1:
time: 176 us; the launch traced here: 175 us
  blocking collectives  86.2 us (49%)
  matrix products  52.1 us (30%)
  other arithmetic  18.9 us (11%)
  starting transfers between devices  12.4 us (7%)
  local copies, waits for them, and re-layouts  5.27 us (3%)
    all_gather x8, blocking collectives, one_axis_at_a_time(): value = jnp.sum(lax.all_gather(value, axis), axis=0)  86.2 us
    dot_general x5, matrix products, attend_block(): jnp.einsum('hqk,khd->qhd', expo.astype(jnp.bfloat16), value_heads, prefer...  15.4 us
    dot_general x5, matrix products, attend_block(): jnp.einsum('qhd,khd->hqk', query_heads, key_heads, preferred_element_type...  15.2 us
    reduce_sum x3, other arithmetic, attend_block(): new_total = running_total * factor + jnp.sum(expo, axis=-1)  14.1 us
    ppermute x4, starting transfers between devices, passed_along(): return lax.ppermute(value, axis, pairs)  12.4 us
    dot_general x5, matrix products, project_pair(): jnp.dot(features, w_value, preferred_element_type=jnp.float32)  8.7 us
    dot_general x5, matrix products, project_pair(): jnp.dot(features, w_key, preferred_element_type=jnp.float32)  8.45 us
    gt x4, local copies, waits for them, and re-layouts, body(): masks[offset + REACH] > 0  4.14 us
  transfers between devices with their start and end apart: 4, of which 0 were waited for; matrix products, arithmetic and copies ran while one was open for 16% of the time, Pallas kernels for 0%

profile of v1, /device:TPU:1, one launch (start us, length us, event | category | flops | bytes accessed | tf_op | source)
XLA Modules:
  0.0 175.4 jit_solution(3743388459334929640)
XLA Ops:
  3.0 2.2 %collective-permute-start.3 = (bf16[512,512]{1,0:T(8,128)(2,1)S(1)}, bf16[512,512]{1,0:T(8,128)(2,1)}, u32[]{:S(2)}, u32[]{:S(2)}) collective-permute-start(bf16[512,512]{1,0:T(8,128)(2,1)S(1)} %fusion.83), channel_id=1, source_target_pairs={{0,2},{1,3},{2,4},{3,5},{4,6},{5,7},{6,8},{7,9},{8,10},{9,11},{10,... | collective-permute-start | bytes 1572872 | tf_op jit(solution)/shard_map/ppermute | solution.py:18
  5.2 9.3 %collective-permute-start.2 = (bf16[512,512]{1,0:T(8,128)(2,1)S(1)}, bf16[512,512]{1,0:T(8,128)(2,1)}, u32[]{:S(2)}, u32[]{:S(2)}) collective-permute-start(bf16[512,512]{1,0:T(8,128)(2,1)S(1)} %fusion.83), channel_id=1, source_target_pairs={{0,126},{1,127},{2,0},{3,1},{4,2},{5,3},{6,4},{7,5},{8,6},{9,7},{1... | collective-permute-start | bytes 1572872 | tf_op jit(solution)/shard_map/ppermute | solution.py:18
  15.5 2.3 %convolution_convert_fusion.8 = bf16[512,512]{0,1:T(8,128)(2,1)} fusion(bf16[512,512]{1,0:T(8,128)(2,1)S(1)} %fusion.83, bf16[512,512]{1,0:T(8,128)(2,1)} %param.16), kind=kOutput, calls=%fused_computation.71 | convolution fusion | flops 268697600 | bytes 1572864 | tf_op jit(solution)/shard_map/dot_general | solution.py:49
  17.8 2.3 %convolution_convert_fusion.9 = bf16[512,512]{0,1:T(8,128)(2,1)} fusion(bf16[512,512]{1,0:T(8,128)(2,1)S(1)} %fusion.83, bf16[512,512]{1,0:T(8,128)(2,1)} %param.15), kind=kOutput, calls=%fused_computation.72 | convolution fusion | flops 268697600 | bytes 1572864 | tf_op jit(solution)/shard_map/dot_general | solution.py:48
  28.4 2.6 %fusion = (f32[8,512]{1,0:T(8,128)S(1)}, f32[8,512,512]{1,2,0:T(8,128)S(1)}) fusion(pred[512,512]{0,1:T(8,128)(4,1)} %copy.22, bf16[512,8,64]{0,2,1:T(8,128)(2,1)S(1)} %bitcast.201, bf16[512,8,64]{0,2,1:T(8,128)(2,1)} %bitcast.206), kind=kOutput, calls=%fused_computation.10 | convolution fusion | flops 274722816 | bytes 9715712 | tf_op jit(solution)/shard_map/qhd,khd->hqk/dot_general | solution.py:32
  38.7 4.7 %fusion.1 = (f32[8,512]{1,0:T(8,128)S(1)}, f32[8,512,512]{1,2,0:T(8,128)}) fusion(pred[512,512]{0,1:T(8,128)(4,1)S(1)} %copy.24, bf16[512,8,64]{0,2,1:T(8,128)(2,1)S(1)} %bitcast.204, bf16[512,8,64]{0,2,1:T(8,128)(2,1)S(1)} %bitcast.210), kind=kOutput, calls=%fused_computation.11 | convolution fusion | flops 274722816 | bytes 9715712 | tf_op jit(solution)/shard_map/qhd,khd->hqk/dot_general | solution.py:32
  44.9 4.9 %fusion.2 = (f32[8,512]{1,0:T(8,128)S(1)}, f32[8,512,512]{1,2,0:T(8,128)}) fusion(pred[512,512]{0,1:T(8,128)(4,1)S(1)} %copy.26, bf16[512,8,64]{0,2,1:T(8,128)(2,1)S(1)} %bitcast.205, bf16[512,8,64]{0,2,1:T(8,128)(2,1)S(1)} %bitcast.207), kind=kOutput, calls=%fused_computation.12 | convolution fusion | flops 274722816 | bytes 9715712 | tf_op jit(solution)/shard_map/qhd,khd->hqk/dot_general | solution.py:32
  49.9 2.7 %fusion.13 = f32[8,512]{1,0:T(8,128)S(1)} fusion(f32[8,512,512]{1,2,0:T(8,128)S(1)} %get-tuple-element.25, f32[8,512]{1,0:T(8,128)S(1)} %get-tuple-element.11, pred[512,512]{0,1:T(8,128)(4,1)} %copy.30), kind=kLoop, calls=%fused_computation.23 | loop fusion | flops 8384512 | bytes 8683520 | tf_op jit(solution)/shard_map/reduce_sum | solution.py:39
  52.6 5.7 %fusion.9 = (f32[8,512]{1,0:T(8,128)S(1)}, f32[8,512]{1,0:T(8,128)S(1)}) fusion(f32[8,512,512]{1,2,0:T(8,128)} %get-tuple-element.29, f32[8,512]{1,0:T(8,128)S(1)} %get-tuple-element.13, pred[512,512]{0,1:T(8,128)(4,1)S(1)} %copy.26, f32[8,512]{1,0:T(8,128)S(1)} %get-tuple-element.12, f32[8,512,512]{1,2,0:T(8,128)S(1)} %get-tuple-element.27, ...), kind=kLoop, calls=%fused_computation.19 | loop fusion | flops 16769024 | bytes 17367040 | tf_op jit(solution)/shard_map/reduce_sum | solution.py:39
  58.3 5.7 %fusion.5 = (f32[8,512]{1,0:T(8,128)S(1)}, f32[8,512]{1,0:T(8,128)S(1)}) fusion(f32[8,512,512]{1,2,0:T(8,128)S(1)} %get-tuple-element.33, f32[8,512]{1,0:T(8,128)S(1)} %get-tuple-element.21, pred[512,512]{0,1:T(8,128)(4,1)S(1)} %copy-done.4, f32[8,512]{1,0:T(8,128)S(1)} %get-tuple-element.14, f32[8,512,512]{1,2,0:T(8,128)} %get-tuple-element.31, ...), kind=kLoop, calls=%fused_computation.15 | loop fusion | flops 16769024 | bytes 17367040 | tf_op jit(solution)/shard_map/reduce_sum | solution.py:39
  64.1 2.3 %fusion.68 = f32[512,8,64]{0,2,1:T(8,128)S(1)} fusion(bf16[512,8,64]{0,2,1:T(8,128)(2,1)S(1)} %bitcast.211, f32[8,512,512]{1,2,0:T(8,128)S(1)} %get-tuple-element.33, f32[8,512]{1,0:T(8,128)S(1)} %get-tuple-element.21, pred[512,512]{0,1:T(8,128)(4,1)S(1)} %copy-done.4, f32[512,8]{0,1:T(8,128)S(1)} %get-tuple-element.19, f32[512,8]{0,1:T(8,128)S(1)} %get-tuple-element.20), kind=kOutput, calls=%fused_computation.58 | convolution fusion | flops 277348352 | bytes 10272768 | tf_op jit(solution)/shard_map/hqk,khd->qhd/dot_general | solution.py:40
  68.2 5.8 %fusion.71 = f32[512,8,64]{0,2,1:T(8,128)S(1)} fusion(f32[512,8,64]{0,2,1:T(8,128)S(1)} %fusion.68, bf16[512,8,64]{0,2,1:T(8,128)(2,1)S(1)} %bitcast.213, f32[8,512,512]{1,2,0:T(8,128)} %get-tuple-element.31, f32[8,512]{1,0:T(8,128)S(1)} %get-tuple-element.14, pred[512,512]{0,1:T(8,128)(4,1)S(1)} %copy.24, f32[512,8]{0,1:T(8,128)S(1)} %get-tuple-element.10), kind=kOutput, calls=%fused_computation.59 | convolution fusion | flops 277348352 | bytes 11304960 | tf_op jit(solution)/shard_map/hqk,khd->qhd/dot_general | solution.py:40
  75.5 2.3 %fusion.74 = f32[512,8,64]{0,2,1:T(8,128)S(1)} fusion(f32[512,8,64]{0,2,1:T(8,128)S(1)} %fusion.71, bf16[512,8,64]{0,2,1:T(8,128)(2,1)S(1)} %bitcast.214, f32[8,512,512]{1,2,0:T(8,128)S(1)} %bitcast.200, f32[8,512]{1,0:T(8,128)S(1)} %get-tuple-element.13, pred[512,512]{0,1:T(8,128)(4,1)S(1)} %copy.26, f32[512,8]{0,1:T(8,128)S(1)} %get-tuple-element.9), kind=kOutput, calls=%fused_computation.60 | convolution fusion | flops 277348352 | bytes 11304960 | tf_op jit(solution)/shard_map/hqk,khd->qhd/dot_general | solution.py:40
  79.4 2.6 %fusion.77 = f32[512,8,64]{0,2,1:T(8,128)S(1)} fusion(f32[512,8,64]{0,2,1:T(8,128)S(1)} %fusion.74, bf16[512,8,64]{0,2,1:T(8,128)(2,1)S(1)} %bitcast.215, f32[8,512,512]{1,2,0:T(8,128)S(1)} %get-tuple-element.27, f32[8,512]{1,0:T(8,128)S(1)} %get-tuple-element.12, pred[512,512]{0,1:T(8,128)(4,1)S(1)} %copy.28, f32[512,8]{0,1:T(8,128)S(1)} %get-tuple-element.8), kind=kOutput, calls=%fused_computation.61 | convolution fusion | flops 277348352 | bytes 11304960 | tf_op jit(solution)/shard_map/hqk,khd->qhd/dot_general | solution.py:40
  83.7 2.4 %divide_convert_fusion = bf16[512,8,64]{0,2,1:T(8,128)(2,1)S(1)} fusion(f32[512,8,64]{0,2,1:T(8,128)S(1)} %fusion.77, bf16[512,8,64]{0,2,1:T(8,128)(2,1)S(1)} %bitcast.212, f32[8,512,512]{1,2,0:T(8,128)S(1)} %get-tuple-element.25, f32[8,512]{1,0:T(8,128)S(1)} %get-tuple-element.11, pred[512,512]{0,1:T(8,128)(4,1)S(1)} %copy-done.6, ...), kind=kOutput, calls=%fused_computation.82 | convolution fusion | flops 277610496 | bytes 10780672 | tf_op jit(solution)/shard_map/hqk,khd->qhd/dot_general | solution.py:40
  86.6 4.7 %all-gather.12 = f32[2,1,512]{2,1,0:T(1,128)S(1)} all-gather(f32[1,1,512]{2,1,0:T(1,128)S(1)} %bitcast.223), channel_id=6, replica_groups=mesh['grp'=2,'blk_0'=2,'blk_1'=8,'blk_2'=4,'blk_3'=2] {'blk_0'}, dimensions={0}, use_global_device_ids=true | all-gather | bytes 6144 | tf_op jit(solution)/shard_map/all_gather | solution.py:23
  91.3 4.7 %all-gather.8 = f32[2,1,512]{2,1,0:T(1,128)S(1)} all-gather(f32[1,1,512]{2,1,0:T(1,128)S(1)} %bitcast.222), channel_id=2, replica_groups=mesh['grp'=2,'blk_0'=2,'blk_1'=8,'blk_2'=4,'blk_3'=2] {'blk_0'}, dimensions={0}, use_global_device_ids=true | all-gather | bytes 6144 | tf_op jit(solution)/shard_map/all_gather | solution.py:23
  96.1 15.6 %all-gather.9 = f32[8,1,512]{2,1,0:T(1,128)S(1)} all-gather(f32[1,1,512]{2,1,0:T(1,128)S(1)} %bitcast.219), channel_id=3, replica_groups=mesh['grp'=2,'blk_0'=2,'blk_1'=8,'blk_2'=4,'blk_3'=2] {'blk_1'}, dimensions={0}, use_global_device_ids=true | all-gather | bytes 18432 | tf_op jit(solution)/shard_map/all_gather | solution.py:23
  111.7 8.1 %all-gather.10 = f32[4,1,512]{2,1,0:T(1,128)S(1)} all-gather(f32[1,1,512]{2,1,0:T(1,128)S(1)} %bitcast.216), channel_id=4, replica_groups=mesh['grp'=2,'blk_0'=2,'blk_1'=8,'blk_2'=4,'blk_3'=2] {'blk_2'}, dimensions={0}, use_global_device_ids=true | all-gather | bytes 10240 | tf_op jit(solution)/shard_map/all_gather | solution.py:23
  119.9 19.0 %all-gather.11 = f32[2,1,512]{2,1,0:T(1,128)S(1)} all-gather(f32[1,1,512]{2,1,0:T(1,128)S(1)} %bitcast.220), channel_id=5, replica_groups=mesh['grp'=2,'blk_0'=2,'blk_1'=8,'blk_2'=4,'blk_3'=2] {'blk_3'}, dimensions={0}, use_global_device_ids=true | all-gather | bytes 6144 | tf_op jit(solution)/shard_map/all_gather | solution.py:23
  138.9 15.9 %all-gather.13 = f32[8,1,512]{2,1,0:T(1,128)S(1)} all-gather(f32[1,1,512]{2,1,0:T(1,128)S(1)} %bitcast.218), channel_id=7, replica_groups=mesh['grp'=2,'blk_0'=2,'blk_1'=8,'blk_2'=4,'blk_3'=2] {'blk_1'}, dimensions={0}, use_global_device_ids=true | all-gather | bytes 18432 | tf_op jit(solution)/shard_map/all_gather | solution.py:23
  154.8 8.1 %all-gather.14 = f32[4,1,512]{2,1,0:T(1,128)S(1)} all-gather(f32[1,1,512]{2,1,0:T(1,128)S(1)} %bitcast.217), channel_id=8, replica_groups=mesh['grp'=2,'blk_0'=2,'blk_1'=8,'blk_2'=4,'blk_3'=2] {'blk_2'}, dimensions={0}, use_global_device_ids=true | all-gather | bytes 10240 | tf_op jit(solution)/shard_map/all_gather | solution.py:23
  163.0 10.0 %all-gather.15 = f32[2,1,512]{2,1,0:T(1,128)S(1)} all-gather(f32[1,1,512]{2,1,0:T(1,128)S(1)} %bitcast.221), channel_id=9, replica_groups=mesh['grp'=2,'blk_0'=2,'blk_1'=8,'blk_2'=4,'blk_3'=2] {'blk_3'}, dimensions={0}, use_global_device_ids=true | all-gather | bytes 6144 | tf_op jit(solution)/shard_map/all_gather | solution.py:23
  173.1 2.3 %fusion.80 = bf16[512,512]{1,0:T(8,128)(2,1)} fusion(f32[512,512]{1,0:T(8,128)S(1)} %get-tuple-element.34, bf16[1024,512]{1,0:T(8,128)(2,1)S(1)} %copy-done, bf16[512,1024]{1,0:T(8,128)(2,1)S(1)} %copy-done.9, f32[512]{0:T(512)S(1)} %copy-done.11, f32[512]{0:T(512)S(1)} %copy-done.12, f32[512]{0:T(512)S(1)} %get-tuple-element.23, f32[512]{0:T(512)S(1)} %get-tuple-element.22), kind=kOutput, calls=%fused_computation.62 | convolution fusion | flops 1080295424 | bytes 3678208 | tf_op jit(solution)/shard_map/dot_general | solution.py:102
  (70 shorter events, 28.6 us)
Async XLA Ops:
  0.0 173.1 %copy-start = (bf16[1024,512]{1,0:T(8,128)(2,1)S(1)}, bf16[1024,512]{1,0:T(8,128)(2,1)}, u32[]{:S(2)}) copy-start(bf16[1024,512]{1,0:T(8,128)(2,1)} %param.21) | copy-start | bytes 3145732
  0.0 21.6 %copy-start.3 = (s32[1,5,512,512]{3,2,1,0:T(8,128)S(1)}, s32[1,5,512,512]{3,2,1,0:T(8,128)}, u32[]{:S(2)}) copy-start(s32[1,5,512,512]{3,2,1,0:T(8,128)} %param.12) | copy-start | bytes 15728644
  3.0 31.1 %collective-permute-start.3 = (bf16[512,512]{1,0:T(8,128)(2,1)S(1)}, bf16[512,512]{1,0:T(8,128)(2,1)}, u32[]{:S(2)}, u32[]{:S(2)}) collective-permute-start(bf16[512,512]{1,0:T(8,128)(2,1)S(1)} %fusion.83), channel_id=1, source_target_pairs={{0,2},{1,3},{2,4},{3,5},{4,6},{5,7},{6,8},{7,9},{8,10},{9,11},{10,... | collective-permute-start | bytes 1572872 | tf_op jit(solution)/shard_map/ppermute | solution.py:18
  5.2 25.8 %collective-permute-start.2 = (bf16[512,512]{1,0:T(8,128)(2,1)S(1)}, bf16[512,512]{1,0:T(8,128)(2,1)}, u32[]{:S(2)}, u32[]{:S(2)}) collective-permute-start(bf16[512,512]{1,0:T(8,128)(2,1)S(1)} %fusion.83), channel_id=1, source_target_pairs={{0,126},{1,127},{2,0},{3,1},{4,2},{5,3},{6,4},{7,5},{8,6},{9,7},{1... | collective-permute-start | bytes 1572872 | tf_op jit(solution)/shard_map/ppermute | solution.py:18
  14.5 28.9 %collective-permute-start.1 = (bf16[512,512]{1,0:T(8,128)(2,1)S(1)}, bf16[512,512]{1,0:T(8,128)(2,1)}, u32[]{:S(2)}, u32[]{:S(2)}) collective-permute-start(bf16[512,512]{1,0:T(8,128)(2,1)S(1)} %fusion.83), channel_id=1, source_target_pairs={{0,1},{1,2},{2,3},{3,4},{4,5},{5,6},{6,7},{7,8},{8,9},{9,10},{10,1... | collective-permute-start | bytes 1572872 | tf_op jit(solution)/shard_map/ppermute | solution.py:18
  14.5 22.7 %collective-permute-start = (bf16[512,512]{1,0:T(8,128)(2,1)S(1)}, bf16[512,512]{1,0:T(8,128)(2,1)}, u32[]{:S(2)}, u32[]{:S(2)}) collective-permute-start(bf16[512,512]{1,0:T(8,128)(2,1)S(1)} %fusion.83), channel_id=1, source_target_pairs={{0,127},{1,0},{2,1},{3,2},{4,3},{5,4},{6,5},{7,6},{8,7},{9,8},{10,... | collective-permute-start | bytes 1572872 | tf_op jit(solution)/shard_map/ppermute | solution.py:18
  21.7 9.4 %copy-start.1 = (bf16[512,512]{1,0:T(8,128)(2,1)S(1)}, bf16[512,512]{1,0:T(8,128)(2,1)}, u32[]{:S(2)}) copy-start(bf16[512,512]{1,0:T(8,128)(2,1)} %param.15) | copy-start | bytes 1572868
  31.0 4.7 %copy-start.5 = (pred[512,512]{0,1:T(8,128)(4,1)S(1)}, pred[512,512]{0,1:T(8,128)(4,1)}, u32[]{:S(2)}) copy-start(pred[512,512]{0,1:T(8,128)(4,1)} %copy.30) | copy-start | bytes 786436
  52.6 5.7 %copy-start.4 = (pred[512,512]{0,1:T(8,128)(4,1)S(1)}, pred[512,512]{0,1:T(8,128)(4,1)}, u32[]{:S(2)}) copy-start(pred[512,512]{0,1:T(8,128)(4,1)} %copy.22) | copy-start | bytes 786436
  58.3 5.8 %copy-start.8 = (bf16[512,512]{0,1:T(8,128)(2,1)S(1)}, bf16[512,512]{0,1:T(8,128)(2,1)}, u32[]{:S(2)}) copy-start(bf16[512,512]{0,1:T(8,128)(2,1)} %convolution_convert_fusion.8) | copy-start | bytes 1572868
  64.1 2.4 %copy-start.2 = (bf16[512,512]{1,0:T(8,128)(2,1)S(1)}, bf16[512,512]{1,0:T(8,128)(2,1)}, u32[]{:S(2)}) copy-start(bf16[512,512]{1,0:T(8,128)(2,1)} %param.16) | copy-start | bytes 1572868
  66.5 9.0 %slice-start = ((s8[8388608]{0:T(1024)(128)(4,1)}), s8[4194304]{0:T(1024)(128)(4,1)S(1)}, s32[]{:S(2)}) async-start(s8[8388608]{0:T(1024)(128)(4,1)} %bitcast.199), calls=%async_computation | async-start | bytes 8388608
  68.1 7.3 %slice-start.1 = ((s8[8388608]{0:T(1024)(128)(4,1)}), s8[4194304]{0:T(1024)(128)(4,1)S(1)}, s32[]{:S(2)}) async-start(s8[8388608]{0:T(1024)(128)(4,1)} %bitcast.199), calls=%async_computation.1 | async-start | bytes 8388608
  77.8 5.8 %copy-start.6 = (pred[512,512]{0,1:T(8,128)(4,1)S(1)}, pred[512,512]{0,1:T(8,128)(4,1)}, u32[]{:S(2)}) copy-start(pred[512,512]{0,1:T(8,128)(4,1)} %copy.30) | copy-start | bytes 786436
  82.0 4.1 %copy-start.7 = (bf16[512,512]{1,0:T(8,128)(2,1)S(1)}, bf16[512,512]{1,0:T(8,128)(2,1)}, u32[]{:S(2)}) copy-start(bf16[512,512]{1,0:T(8,128)(2,1)} %param.11) | copy-start | bytes 1572868
  82.0 4.1 %copy-start.10 = (bf16[512,512]{1,0:T(8,128)(2,1)S(1)}, bf16[512,512]{1,0:T(8,128)(2,1)}, u32[]{:S(2)}) copy-start(bf16[512,512]{1,0:T(8,128)(2,1)} %param.17) | copy-start | bytes 1572868
  83.6 89.5 %copy-start.9 = (bf16[512,1024]{1,0:T(8,128)(2,1)S(1)}, bf16[512,1024]{1,0:T(8,128)(2,1)}, u32[]{:S(2)}) copy-start(bf16[512,1024]{1,0:T(8,128)(2,1)} %param.20) | copy-start | bytes 3145732
  83.6 89.5 %copy-start.11 = (f32[512]{0:T(512)S(1)}, f32[512]{0:T(512)}, u32[]{:S(2)}) copy-start(f32[512]{0:T(512)} %param.19) | copy-start | bytes 6148
  83.7 89.5 %copy-start.12 = (f32[512]{0:T(512)S(1)}, f32[512]{0:T(512)}, u32[]{:S(2)}) copy-start(f32[512]{0:T(512)} %param.18) | copy-start | bytes 6148
